TPU v7x, 32 devices: a whole 2x2x4 slice. The times are simulated.
32 devices in a mesh: gx: 4 (over z), gy: 4 (over y, core), af: 2 (over x).
Axes of the slice: x: 2, y: 2, z: 4, core: 2. Of those that a mesh axis runs over, the one named last changes fastest.
Arguments:
- points: bfloat16 [1024, 256], P(('gx', 'gy'), 'af'), may hold values from -12 to 12
- targets: float32 [1024, 16], P(('gx', 'gy')), may hold values from -6 to 6
Outputs:
- solution: float32 [1024, 16], P(('gx', 'gy'))
- residual: float32 [1024, 16], P(('gx', 'gy'))
All inputs are finite; a program needn't handle non-finite values.
Results may differ from a plain program's by a relative error of at most 0.025.
Values may be sent and summed in bfloat16 or wider, within the bound.
No kernel may reach another device: no remote copies, remote signals or barrier semaphores. Data moves between devices by JAX's collectives and lax.ppermute only.
A program may use at most 64 MiB of HBM per device.

v0:
```python
import functools
import math

import jax
import jax.numpy as jnp
from jax import lax
from jax.experimental import pallas as pl
from jax.experimental.pallas import tpu as pltpu
from jax.sharding import PartitionSpec as P


ITERS = 2


def point_norms(block):
    wide_block = block.astype(jnp.float32)
    return jnp.sum(wide_block * wide_block, axis=1)


def kernel_times(row_slab, slab_norms, col_slab, col_slab_norms, col_vector, scale):
    inner = lax.dot_general(
        row_slab, col_slab, (((1,), (1,)), ((), ())), preferred_element_type=jnp.float32
    )
    distance = slab_norms[:, None] + col_slab_norms[None, :] - 2.0 * inner
    kernel = jnp.exp(-scale * distance).astype(jnp.bfloat16)
    return jnp.dot(kernel, col_vector, preferred_element_type=jnp.float32)


def split_size(count):
    block_size = count
    while block_size > 1024 and block_size % 2 == 0:
        block_size = block_size // 2
    return block_size


def split_local(points, targets):
    whole_feat = lax.all_gather(points, "af", axis=1, tiled=True)
    norms = point_norms(whole_feat)
    half_rows = whole_feat.shape[0] // 2
    start_row = lax.axis_index("af") * half_rows
    my_points = lax.dynamic_slice_in_dim(whole_feat, start_row, half_rows, 0)
    scale = 0.5 / whole_feat.shape[1]
    stored_points = lax.all_gather(my_points, ("gx", "gy"), axis=0, tiled=True)
    stored_norms = point_norms(stored_points)

    def operate(vector):
        lowered = vector.astype(jnp.bfloat16)
        my_vector = lax.dynamic_slice_in_dim(lowered, start_row, half_rows, 0)
        empty = jnp.zeros(vector.shape, jnp.float32)
        piece = lax.all_gather(my_vector, ("gx", "gy"), axis=0, tiled=True)
        count = piece.shape[0]
        block_size = split_size(count)

        def one_block(carry, index):
            offset = index * block_size
            col_slab = lax.dynamic_slice_in_dim(stored_points, offset, block_size, 0)
            col_slab_norms = lax.dynamic_slice_in_dim(stored_norms, offset, block_size, 0)
            vector_slab = lax.dynamic_slice_in_dim(piece, offset, block_size, 0)
            return (
                carry
                + kernel_times(whole_feat, norms, col_slab, col_slab_norms, vector_slab, scale),
                None,
            )

        result, _ = lax.scan(one_block, empty, jnp.arange(count // block_size, dtype=jnp.int32))
        return lax.psum(result, "af") + 0.1 * vector

    def two_products(values, image):
        return lax.psum(
            (jnp.sum(values * values, axis=0), jnp.sum(values * image, axis=0)), ("gx", "gy")
        )

    solution = jnp.zeros_like(targets)
    residual = targets
    image = operate(residual)
    norm_now, product = two_products(residual, image)
    alpha = norm_now / product
    direction = residual
    along = image
    for step in range(ITERS):
        solution = solution + alpha * direction
        residual = residual - alpha * along
        if step + 1 < ITERS:
            image = operate(residual)
            norm_next, product = two_products(residual, image)
            ratio = norm_next / norm_now
            alpha = norm_next / (product - ratio * norm_next / alpha)
            direction = residual + ratio * direction
            along = image + ratio * along
            norm_now = norm_next
    return (solution, residual)


AXES = ("gx", "gy", "af")
LANES = 128
PANEL = 4 * LANES
EYE_COST = pl.CostEstimate(flops=20000000, transcendentals=0, bytes_accessed=65536)
KERNEL_BYTES = 8 * 1024 * 1024


def pack_kernel(points, turned, own, packed):
    wide = turned[...]
    high = wide.astype(jnp.bfloat16)
    low = (wide - high.astype(jnp.float32)).astype(jnp.bfloat16)
    both = jnp.concatenate([high, low], axis=1)
    packed[...] = both
    own[: points.shape[0], :] = points[...]
    own[points.shape[0] :, :] = both


def row_dot(a, b):
    return lax.dot_general(a, b, (((1,), (1,)), ((), ())), preferred_element_type=jnp.float32)


def plain_dot(a, b):
    return jnp.dot(a, b, preferred_element_type=jnp.float32)


def turn_of(features):
    return math.log2(math.e) * 0.5 / features


def unpack(blocks, rows, columns, groups, coords, parts):
    group = blocks * rows
    packed = []
    for index, (main, other) in enumerate(groups):
        width = main.shape[1]
        coords[index * group : (index + 1) * group, :width] = main[:group, :]
        coords[index * group : (index + 1) * group, width:] = other[...]
        for block in range(blocks):
            both = main[group + block * columns : group + (block + 1) * columns, :]
            packed.append(both.astype(jnp.float32))
    left = lax.broadcasted_iota(jnp.int32, packed[0].shape, 1) < rows
    for k in range(len(packed) // 2):
        one, two = packed[2 * k : 2 * k + 2]
        high = jnp.where(left, one, pltpu.roll(two, rows, 1))
        low = jnp.where(left, pltpu.roll(one, rows, 1), two)
        stacked = jnp.concatenate([high, low], axis=0).astype(jnp.bfloat16)
        parts[:, k * LANES : (k + 1) * LANES] = stacked


def eye_kernel(eye):
    rows = lax.broadcasted_iota(jnp.int32, eye.shape, 0)
    eye[...] = (rows == lax.broadcasted_iota(jnp.int32, eye.shape, 1)).astype(jnp.float32)


def scaled_norms(coords, start, down, along, eye):
    turn = turn_of(coords.shape[1])
    wide = coords[start : start + PANEL, :].astype(jnp.float32)
    column = -turn * jnp.sum(wide * wide, axis=1, keepdims=True)
    spread = jnp.broadcast_to(column, (PANEL, LANES))
    down[start : start + PANEL, :] = spread
    for k in range(PANEL // LANES):
        picked = eye[...] * spread[k * LANES : (k + 1) * LANES, :]
        row = jnp.sum(picked, axis=0, keepdims=True)
        first = start + k * LANES
        along[:, first : first + LANES] = jnp.broadcast_to(row, (8, LANES))


def kernel_columns(coords, down, along, kernel, begin, end, start):
    turn = turn_of(coords.shape[1])
    inner = row_dot(coords[begin:end, :], coords[start : start + PANEL, :])
    column = down[begin:end, :]
    column = jnp.concatenate([column] * (PANEL // LANES), axis=1)
    power = (2.0 * turn) * inner + column + along[:1, start : start + PANEL]
    kernel[begin:end, start : start + PANEL] = jnp.exp2(power).astype(jnp.bfloat16)


def join(parts):
    half = parts.shape[0] // 2
    return parts[:half, :] + parts[half:, :]


def own_kernel(blocks, rows, count, *refs):
    eye, coords, down, along, kernel, parts, image = refs[count:]
    groups = [(refs[k], refs[k + 1]) for k in range(0, count, 2)]
    unpack(blocks, rows, parts.shape[0] // 2, groups, coords, parts)
    half = coords.shape[0]
    for i in range(0, half, PANEL):
        scaled_norms(coords, i, down, along, eye)
    for j in range(0, half, PANEL):
        kernel_columns(coords, down, along, kernel, 0, half, j)
        image[:, j : j + PANEL] = plain_dot(parts[...], kernel[:, j : j + PANEL])


def solve_kernel(blocks, rows, count, *refs):
    eye, own, own_down, own_along, own_block, own_parts, own_image = refs[count : count + 7]
    solution_ref, residual_ref = refs[count + 7 : count + 9]
    coords, down, along, kernel, parts = refs[count + 9 :]
    groups = [(refs[k], refs[k + 1]) for k in range(0, count, 2)]
    half = own.shape[0]
    whole = 2 * half
    unpack(
        blocks, rows, parts.shape[0] // 2, groups, coords.at[half:, :], parts.at[:, half:]
    )
    coords[:half, :] = own[...]
    down[:half, :] = own_down[...]
    along[:, :half] = own_along[...]
    parts[:, :half] = own_parts[...]
    for i in range(half, whole, PANEL):
        scaled_norms(coords, i, down, along, eye)
    for j in range(0, half, PANEL):
        kernel_columns(coords, down, along, kernel, half, whole, j)
    for j in range(half, whole, PANEL):
        kernel_columns(coords, down, along, kernel, 0, whole, j)
    products = [
        own_image[...] + plain_dot(parts[:, half:], kernel[half:, :half]),
        plain_dot(parts[...], kernel[:, half:]),
    ]
    kernel[:half, :half] = own_block[...]
    targets = join(parts[...].astype(jnp.float32))

    def total_of(a, b):
        return jnp.sum(a * b, axis=1, keepdims=True)

    image = join(jnp.concatenate(products, axis=1)) + 0.1 * targets
    high = image.astype(jnp.bfloat16)
    low = (image - high.astype(jnp.float32)).astype(jnp.bfloat16)
    stacked = jnp.concatenate([high, low], axis=0)
    again = join(plain_dot(stacked, kernel[...])) + 0.1 * image
    norm_first = total_of(targets, targets)
    alpha = norm_first / total_of(targets, image)
    residual = targets - alpha * image
    norm_next = total_of(residual, residual)
    ratio = norm_next / norm_first
    direction = residual + ratio * targets
    along_direction = (1.0 + ratio) * image - alpha * again
    step = norm_next / total_of(direction, along_direction)
    solution_ref[...] = (alpha * targets + step * direction)[:, :rows]
    residual_ref[...] = (residual - step * along_direction)[:, :rows]


def swap(array, sizes, flips):
    pairs = []
    for place in range(math.prod(sizes)):
        rest, far, weight = place, 0, 1
        for size, flip in zip(reversed(sizes), reversed(flips)):
            far += ((rest % size) ^ flip) * weight
            rest, weight = rest // size, weight * size
        pairs.append((place, far))
    return lax.ppermute(array, AXES, pairs)


def in_vmem(arrays):
    return [pltpu.with_memory_space_constraint(array, pltpu.VMEM) for array in arrays]


def whole_local(sizes, points, targets):
    across, along, features = sizes
    rows = points.shape[0]
    columns = targets.shape[1]
    vmem = pl.BlockSpec(memory_space=pltpu.VMEM)
    eye = pl.pallas_call(
        eye_kernel,
        out_shape=pltpu.VMEM((LANES, LANES), jnp.float32),
        out_specs=vmem,
        cost_estimate=EYE_COST,
    )()
    early = across // 2
    early_points = swap(points, sizes, (early, 0, 0))
    packed_shape = (columns, 2 * rows)
    own, packed = pl.pallas_call(
        pack_kernel,
        out_shape=(
            pltpu.VMEM((rows + columns, LANES), jnp.bfloat16),
            pltpu.VMEM(packed_shape, jnp.bfloat16),
        ),
        in_specs=[vmem, vmem],
        out_specs=(vmem, vmem),
    )(*in_vmem([points, targets.T]))
    blocks = {0: own}
    for k in reversed(range(1, across)):
        if k != early:
            blocks[k] = swap(own, sizes, (k, 0, 0))
    late = swap(packed, sizes, (early, 0, 0))
    order = range(across)
    coords = [early_points if k == early else blocks[k][:rows] for k in order]
    coords = jnp.concatenate(coords, axis=0)
    parts = [late if k == early else blocks[k][rows:] for k in order]
    main = jnp.concatenate([coords, *parts], axis=0)
    moves = [(y, x) for y in range(0, along, 2) for x in range(features)]
    got = {}
    for y, x in reversed(moves):
        if (y, x) == (0, 0):
            got[y, x] = main
        else:
            got[y, x] = swap(coords if x else main, sizes, (0, y, x))
    ours = [got[move] for move in moves]
    theirs = [swap(block, sizes, (0, 1, 0)) for block in ours]
    half = rows * across * along // 2
    width = points.shape[1] * features
    f32, bf16 = jnp.float32, jnp.bfloat16
    vmem = pl.BlockSpec(memory_space=pltpu.VMEM)
    kept = (
        pltpu.VMEM((half, width), bf16),
        pltpu.VMEM((half, LANES), f32),
        pltpu.VMEM((8, half), f32),
        pltpu.VMEM((half, half), bf16),
        pltpu.VMEM((2 * columns, half), bf16),
        pltpu.VMEM((2 * columns, half), f32),
    )
    held = pl.pallas_call(
        functools.partial(own_kernel, across, rows, len(ours)),
        out_shape=kept,
        in_specs=[vmem] * (len(ours) + 1),
        out_specs=[vmem] * len(kept),
        cost_estimate=pl.CostEstimate(
            flops=2 * half * half * (width + LANES),
            transcendentals=half * half,
            bytes_accessed=2 * half * width,
        ),
    )(*in_vmem([*ours, eye]))
    out = jax.ShapeDtypeStruct((columns, rows), f32)
    solution, residual = pl.pallas_call(
        functools.partial(solve_kernel, across, rows, len(theirs)),
        out_shape=(out, out),
        in_specs=[vmem] * (len(theirs) + 1 + len(kept)),
        out_specs=(vmem, vmem),
        scratch_shapes=[
            pltpu.VMEM((2 * half, width), bf16),
            pltpu.VMEM((2 * half, LANES), f32),
            pltpu.VMEM((8, 2 * half), f32),
            pltpu.VMEM((2 * half, 2 * half), bf16),
            pltpu.VMEM((2 * columns, 2 * half), bf16),
        ],
        cost_estimate=pl.CostEstimate(
            flops=6 * half * half * (width + LANES),
            transcendentals=3 * half * half,
            bytes_accessed=2 * half * width,
        ),
    )(*in_vmem([*theirs, eye, *held]))
    return solution.T, residual.T


def fits_whole(sizes, points, targets):
    across, along, features = sizes
    rows, width = points.shape
    count = rows * across * along
    powers = all(size & (size - 1) == 0 for size in sizes)
    return (
        powers
        and along > 1
        and features == 2
        and 2 * rows == LANES
        and width == LANES
        and targets.shape[1] == 16
        and count % (2 * PANEL) == 0
        and 2 * count * count <= KERNEL_BYTES
        and ITERS == 2
    )


def local(sizes, points, targets):
    if fits_whole(sizes, points, targets):
        return whole_local(sizes, points, targets)
    return split_local(points, targets)


def solution(mesh):
    placed = (P(("gx", "gy"), "af"), P(("gx", "gy"), None))
    sizes = tuple(mesh.shape[axis] for axis in AXES)
    return jax.shard_map(
        functools.partial(local, sizes),
        mesh=mesh,
        in_specs=placed,
        out_specs=(P(("gx", "gy"), None), P(("gx", "gy"), None)),
        check_vma=False,
    )
```

profile of v0, /device:TPU:0, one launch (start us, length us, event | category | flops | bytes accessed | tf_op | source)
XLA Modules:
  0.0 24.1 jit_solution(12678187227962561766)
XLA Ops:
  0.6 4.1 %collective-permute-start.1 = (bf16[64,128]{1,0:T(8,128)(2,1)}, bf16[64,128]{1,0:T(8,128)(2,1)S(1)}, u32[]{:S(2)}, u32[]{:S(2)}) collective-permute-start(bf16[64,128]{1,0:T(8,128)(2,1)} %points.1), channel_id=1, source_target_pairs={{0,16},{1,17},{2,18},{3,19},{4,20},{5,21},{6,22},{7,23},{8,24},{9,... | collective-permute-start | bytes 49160 | tf_op jit(solution)/shard_map/ppermute | solution.py:241
  4.8 0.0 copy-start
  4.8 0.7 %copy-done = bf16[64,128]{1,0:T(8,128)(2,1)S(1)} copy-done((bf16[64,128]{1,0:T(8,128)(2,1)S(1)}, bf16[64,128]{1,0:T(8,128)(2,1)}, u32[]{:S(2)}) %copy-start) | copy-done | bytes 16408
  5.5 0.0 copy-start.1
  5.5 0.7 %copy-done.1 = f32[64,16]{0,1:T(8,128)S(1)} copy-done((f32[64,16]{0,1:T(8,128)S(1)}, f32[64,16]{0,1:T(8,128)}, u32[]{:S(2)}) %copy-start.1) | copy-done | bytes 4120
  6.2 0.1 shard_map.41
  6.3 1.6 %collective-permute-start = (bf16[80,128]{1,0:T(8,128)(2,1)S(1)}, bf16[80,128]{1,0:T(8,128)(2,1)S(1)}, u32[]{:S(2)}, u32[]{:S(2)}) collective-permute-start(bf16[80,128]{1,0:T(8,128)(2,1)S(1)} %get-tuple-element.12), channel_id=1, source_target_pairs={{0,8},{1,9},{2,10},{3,11},{4,12},{5,13},{6,14},{7,15},{8,0},{9,1},... | collective-permute-start | bytes 61448 | tf_op jit(solution)/shard_map/ppermute | solution.py:241
  7.9 0.0 collective-permute-start.2
  7.9 1.9 %collective-permute-start.3 = (bf16[16,128]{1,0:T(8,128)(2,1)S(1)}, bf16[16,128]{1,0:T(8,128)(2,1)S(1)}, u32[]{:S(2)}, u32[]{:S(2)}) collective-permute-start(bf16[16,128]{1,0:T(8,128)(2,1)S(1)} %get-tuple-element.13), channel_id=1, source_target_pairs={{0,16},{1,17},{2,18},{3,19},{4,20},{5,21},{6,22},{7,23},{8,24},{9,... | collective-permute-start | bytes 12296 | tf_op jit(solution)/shard_map/ppermute | solution.py:241
  9.8 0.3 %collective-permute-done = bf16[80,128]{1,0:T(8,128)(2,1)S(1)} collective-permute-done((bf16[80,128]{1,0:T(8,128)(2,1)S(1)}, bf16[80,128]{1,0:T(8,128)(2,1)S(1)}, u32[]{:S(2)}, u32[]{:S(2)}) %collective-permute-start) | collective-permute-done | bytes 20512 | tf_op jit(solution)/shard_map/ppermute | solution.py:241
  10.1 0.0 collective-permute-done.1
  10.1 3.3 %collective-permute-done.2 = bf16[80,128]{1,0:T(8,128)(2,1)S(1)} collective-permute-done((bf16[80,128]{1,0:T(8,128)(2,1)S(1)}, bf16[80,128]{1,0:T(8,128)(2,1)S(1)}, u32[]{:S(2)}, u32[]{:S(2)}) %collective-permute-start.2) | collective-permute-done | bytes 20512 | tf_op jit(solution)/shard_map/ppermute | solution.py:241
  13.5 0.0 collective-permute-done.3
  13.5 1.6 %collective-permute-start.7 = (bf16[320,128]{1,0:T(8,128)(2,1)S(1)}, bf16[320,128]{1,0:T(8,128)(2,1)S(1)}, u32[]{:S(2)}, u32[]{:S(2)}) collective-permute-start(bf16[320,128]{1,0:T(8,128)(2,1)S(1)} %constant_dynamic-update-slice_fusion.refs_0_), channel_id=1, source_target_pairs={{0,4},{1,5},{2,6},{3,7},{4,0},{5,1},{6,2},{7,3},{8,12},{9,13},{10,... | collective-permute-start | bytes 245768 | tf_op jit(solution)/shard_map/ppermute | solution.py:241
  15.1 1.4 %collective-permute-start.9 = (bf16[256,128]{1,0:T(8,128)(2,1)S(1)}, bf16[256,128]{1,0:T(8,128)(2,1)S(1)}, u32[]{:S(2)}, u32[]{:S(2)}) collective-permute-start(bf16[256,128]{1,0:T(8,128)(2,1)S(1)} %pad_maximum_fusion), channel_id=1, source_target_pairs={{0,5},{1,4},{2,7},{3,6},{4,1},{5,0},{6,3},{7,2},{8,13},{9,12},{10,... | collective-permute-start | bytes 196616 | tf_op jit(solution)/shard_map/ppermute | solution.py:241
  16.5 0.5 %collective-permute-start.5 = (bf16[256,128]{1,0:T(8,128)(2,1)S(1)}, bf16[256,128]{1,0:T(8,128)(2,1)S(1)}, u32[]{:S(2)}, u32[]{:S(2)}) collective-permute-start(bf16[256,128]{1,0:T(8,128)(2,1)S(1)} %pad_maximum_fusion), channel_id=1, source_target_pairs={{0,1},{1,0},{2,3},{3,2},{4,5},{5,4},{6,7},{7,6},{8,9},{9,8},{10,11... | collective-permute-start | bytes 196616 | tf_op jit(solution)/shard_map/ppermute | solution.py:241
  17.1 0.0 collective-permute-start.4
  17.1 0.9 %collective-permute-done.7.refs_2_ = bf16[320,128]{1,0:T(8,128)(2,1)S(1)} collective-permute-done((bf16[320,128]{1,0:T(8,128)(2,1)S(1)}, bf16[320,128]{1,0:T(8,128)(2,1)S(1)}, u32[]{:S(2)}, u32[]{:S(2)}) %collective-permute-start.7) | collective-permute-done | bytes 81952 | tf_op jit(solution)/shard_map/ppermute | solution.py:241
  18.0 0.0 collective-permute-start.8
  18.0 2.2 %collective-permute-done.9.refs_3_ = bf16[256,128]{1,0:T(8,128)(2,1)S(1)} collective-permute-done((bf16[256,128]{1,0:T(8,128)(2,1)S(1)}, bf16[256,128]{1,0:T(8,128)(2,1)S(1)}, u32[]{:S(2)}, u32[]{:S(2)}) %collective-permute-start.9) | collective-permute-done | bytes 65568 | tf_op jit(solution)/shard_map/ppermute | solution.py:241
  20.3 0.0 collective-permute-start.10
  20.3 0.5 %collective-permute-done.5.refs_1_ = bf16[256,128]{1,0:T(8,128)(2,1)S(1)} collective-permute-done((bf16[256,128]{1,0:T(8,128)(2,1)S(1)}, bf16[256,128]{1,0:T(8,128)(2,1)S(1)}, u32[]{:S(2)}, u32[]{:S(2)}) %collective-permute-start.5) | collective-permute-done | bytes 65568 | tf_op jit(solution)/shard_map/ppermute | solution.py:241
  20.8 0.0 collective-permute-start.6
  20.8 0.6 %shard_map.43 = (bf16[512,256]{1,0:T(8,128)(2,1)S(1)}, f32[512,128]{1,0:T(8,128)S(1)}, f32[8,512]{1,0:T(8,128)S(1)}, bf16[512,512]{1,0:T(8,128)(2,1)S(1)}, bf16[...) custom-call(bf16[320,128]{1,0:T(8,128)(2,1)S(1)} %constant_dynamic-update-slice_fusion.refs_0_, ...), custom_call_target="tpu_custom_call" | custom-call | flops 201326592 | bytes 262144 | tf_op jit(solution)/shard_map/pallas_call | solution.py:302
  21.4 0.0 collective-permute-done.4.refs_0_
  21.4 0.1 collective-permute-done.10.refs_3_
  21.5 0.5 %collective-permute-done.6.refs_1_ = bf16[256,128]{1,0:T(8,128)(2,1)S(1)} collective-permute-done((bf16[256,128]{1,0:T(8,128)(2,1)S(1)}, bf16[256,128]{1,0:T(8,128)(2,1)S(1)}, u32[]{:S(2)}, u32[]{:S(2)}) %collective-permute-start.6) | collective-permute-done | bytes 65568 | tf_op jit(solution)/shard_map/ppermute | solution.py:241
  22.0 0.0 collective-permute-done.8.refs_2_
  22.1 2.1 %shard_map.44 = (f32[16,64]{1,0:T(8,128)}, f32[16,64]{1,0:T(8,128)}) custom-call(bf16[320,128]{1,0:T(8,128)(2,1)S(1)} %collective-permute-done.4.refs_0_, bf16[256,128]{1,0:T(8,128)(2,1)S(1)} %collective-permute-done.6.refs_1_, bf16[320,128]{1,0:T(8,128)(2,1)S(1)} %collective-permute-done.8.refs_2_, bf16[256,128]{1,0:T(8,128)(2,1)S(1)} %collective-permute-done.10.refs_3_, ...), custom_call_target="tpu_custom_call" | custom-call | flops 603979776 | bytes 262144 | tf_op jit(solution)/shard_map/pallas_call | solution.py:314
  (10 shorter events, 0.1 us)
Async XLA Ops:
  0.6 9.5 %collective-permute-start.1 = (bf16[64,128]{1,0:T(8,128)(2,1)}, bf16[64,128]{1,0:T(8,128)(2,1)S(1)}, u32[]{:S(2)}, u32[]{:S(2)}) collective-permute-start(bf16[64,128]{1,0:T(8,128)(2,1)} %points.1), channel_id=1, source_target_pairs={{0,16},{1,17},{2,18},{3,19},{4,20},{5,21},{6,22},{7,23},{8,24},{9,... | collective-permute-start | bytes 49160 | tf_op jit(solution)/shard_map/ppermute | solution.py:241
  4.8 0.8 %copy-start = (bf16[64,128]{1,0:T(8,128)(2,1)S(1)}, bf16[64,128]{1,0:T(8,128)(2,1)}, u32[]{:S(2)}) copy-start(bf16[64,128]{1,0:T(8,128)(2,1)} %points.1) | copy-start | bytes 49156
  5.5 0.7 %copy-start.1 = (f32[64,16]{0,1:T(8,128)S(1)}, f32[64,16]{0,1:T(8,128)}, u32[]{:S(2)}) copy-start(f32[64,16]{0,1:T(8,128)} %param.3) | copy-start | bytes 12292
  6.3 3.8 %collective-permute-start = (bf16[80,128]{1,0:T(8,128)(2,1)S(1)}, bf16[80,128]{1,0:T(8,128)(2,1)S(1)}, u32[]{:S(2)}, u32[]{:S(2)}) collective-permute-start(bf16[80,128]{1,0:T(8,128)(2,1)S(1)} %get-tuple-element.12), channel_id=1, source_target_pairs={{0,8},{1,9},{2,10},{3,11},{4,12},{5,13},{6,14},{7,15},{8,0},{9,1},... | collective-permute-start | bytes 61448 | tf_op jit(solution)/shard_map/ppermute | solution.py:241
  7.9 5.6 %collective-permute-start.2 = (bf16[80,128]{1,0:T(8,128)(2,1)S(1)}, bf16[80,128]{1,0:T(8,128)(2,1)S(1)}, u32[]{:S(2)}, u32[]{:S(2)}) collective-permute-start(bf16[80,128]{1,0:T(8,128)(2,1)S(1)} %get-tuple-element.12), channel_id=1, source_target_pairs={{0,24},{1,25},{2,26},{3,27},{4,28},{5,29},{6,30},{7,31},{8,16},{9,... | collective-permute-start | bytes 61448 | tf_op jit(solution)/shard_map/ppermute | solution.py:241
  7.9 5.6 %collective-permute-start.3 = (bf16[16,128]{1,0:T(8,128)(2,1)S(1)}, bf16[16,128]{1,0:T(8,128)(2,1)S(1)}, u32[]{:S(2)}, u32[]{:S(2)}) collective-permute-start(bf16[16,128]{1,0:T(8,128)(2,1)S(1)} %get-tuple-element.13), channel_id=1, source_target_pairs={{0,16},{1,17},{2,18},{3,19},{4,20},{5,21},{6,22},{7,23},{8,24},{9,... | collective-permute-start | bytes 12296 | tf_op jit(solution)/shard_map/ppermute | solution.py:241
  13.5 4.5 %collective-permute-start.7 = (bf16[320,128]{1,0:T(8,128)(2,1)S(1)}, bf16[320,128]{1,0:T(8,128)(2,1)S(1)}, u32[]{:S(2)}, u32[]{:S(2)}) collective-permute-start(bf16[320,128]{1,0:T(8,128)(2,1)S(1)} %constant_dynamic-update-slice_fusion.refs_0_), channel_id=1, source_target_pairs={{0,4},{1,5},{2,6},{3,7},{4,0},{5,1},{6,2},{7,3},{8,12},{9,13},{10,... | collective-permute-start | bytes 245768 | tf_op jit(solution)/shard_map/ppermute | solution.py:241
  15.1 5.2 %collective-permute-start.9 = (bf16[256,128]{1,0:T(8,128)(2,1)S(1)}, bf16[256,128]{1,0:T(8,128)(2,1)S(1)}, u32[]{:S(2)}, u32[]{:S(2)}) collective-permute-start(bf16[256,128]{1,0:T(8,128)(2,1)S(1)} %pad_maximum_fusion), channel_id=1, source_target_pairs={{0,5},{1,4},{2,7},{3,6},{4,1},{5,0},{6,3},{7,2},{8,13},{9,12},{10,... | collective-permute-start | bytes 196616 | tf_op jit(solution)/shard_map/ppermute | solution.py:241
  16.5 4.3 %collective-permute-start.5 = (bf16[256,128]{1,0:T(8,128)(2,1)S(1)}, bf16[256,128]{1,0:T(8,128)(2,1)S(1)}, u32[]{:S(2)}, u32[]{:S(2)}) collective-permute-start(bf16[256,128]{1,0:T(8,128)(2,1)S(1)} %pad_maximum_fusion), channel_id=1, source_target_pairs={{0,1},{1,0},{2,3},{3,2},{4,5},{5,4},{6,7},{7,6},{8,9},{9,8},{10,11... | collective-permute-start | bytes 196616 | tf_op jit(solution)/shard_map/ppermute | solution.py:241
  17.1 4.3 %collective-permute-start.4 = (bf16[320,128]{1,0:T(8,128)(2,1)S(1)}, bf16[320,128]{1,0:T(8,128)(2,1)S(1)}, u32[]{:S(2)}, u32[]{:S(2)}) collective-permute-start(bf16[320,128]{1,0:T(8,128)(2,1)S(1)} %constant_dynamic-update-slice_fusion.refs_0_), channel_id=1, source_target_pairs={{0,2},{1,3},{2,0},{3,1},{4,6},{5,7},{6,4},{7,5},{8,10},{9,11},{10,... | collective-permute-start | bytes 245768 | tf_op jit(solution)/shard_map/ppermute | solution.py:241
  18.0 4.0 %collective-permute-start.8 = (bf16[320,128]{1,0:T(8,128)(2,1)S(1)}, bf16[320,128]{1,0:T(8,128)(2,1)S(1)}, u32[]{:S(2)}, u32[]{:S(2)}) collective-permute-start(bf16[320,128]{1,0:T(8,128)(2,1)S(1)} %collective-permute-done.7.refs_2_), channel_id=1, source_target_pairs={{0,2},{1,3},{2,0},{3,1},{4,6},{5,7},{6,4},{7,5},{8,10},{9,11},{10,... | collective-permute-start | bytes 245768 | tf_op jit(solution)/shard_map/ppermute | solution.py:241
  20.3 1.3 %collective-permute-start.10 = (bf16[256,128]{1,0:T(8,128)(2,1)S(1)}, bf16[256,128]{1,0:T(8,128)(2,1)S(1)}, u32[]{:S(2)}, u32[]{:S(2)}) collective-permute-start(bf16[256,128]{1,0:T(8,128)(2,1)S(1)} %collective-permute-done.9.refs_3_), channel_id=1, source_target_pairs={{0,2},{1,3},{2,0},{3,1},{4,6},{5,7},{6,4},{7,5},{8,10},{9,11},{10,... | collective-permute-start | bytes 196616 | tf_op jit(solution)/shard_map/ppermute | solution.py:241
  20.8 1.3 %collective-permute-start.6 = (bf16[256,128]{1,0:T(8,128)(2,1)S(1)}, bf16[256,128]{1,0:T(8,128)(2,1)S(1)}, u32[]{:S(2)}, u32[]{:S(2)}) collective-permute-start(bf16[256,128]{1,0:T(8,128)(2,1)S(1)} %collective-permute-done.5.refs_1_), channel_id=1, source_target_pairs={{0,2},{1,3},{2,0},{3,1},{4,6},{5,7},{6,4},{7,5},{8,10},{9,11},{10,... | collective-permute-start | bytes 196616 | tf_op jit(solution)/shard_map/ppermute | solution.py:241
where the time goes:
time: 24.4 us; the launch traced here: 24.1 us
  starting transfers between devices  11.2 us (46%)
  waiting for transfers between devices  8.04 us (33%)
  Pallas kernels  2.73 us (11%)
  local copies, waits for them, and re-layouts  1.51 us (6%)
  between operations  0.67 us (3%)
    ppermute x11, starting transfers between devices, swap(): return lax.ppermute(array, AXES, pairs)  11.2 us
    ppermute x11, waiting for transfers between devices, swap(): return lax.ppermute(array, AXES, pairs)  8.04 us
    pallas_call x1, Pallas kernels, whole_local(): pl.pallas_call(functools.partial(solve_kernel, across, rows, len(theirs))...  2.08 us
    unnamed x8, local copies, waits for them, and re-layouts  1.48 us
    pallas_call x1, Pallas kernels, whole_local(): pl.pallas_call(functools.partial(own_kernel, across, rows, len(ours)), ou...  0.56 us
  transfers between devices with their start and end apart: 11, of which 7 were waited for; matrix products, arithmetic and copies ran while one was open for 0% of the time, Pallas kernels for 3%

commit v1 on v0

--- a/solution.py
+++ b/solution.py
@@ -157,13 +157,13 @@
         along[:, first : first + LANES] = jnp.broadcast_to(row, (8, LANES))
 
 
-def kernel_columns(coords, down, along, kernel, begin, end, start):
+def kernel_columns(coords, down, along, kernel, begin, end, start, size=PANEL):
     turn = turn_of(coords.shape[1])
-    inner = row_dot(coords[begin:end, :], coords[start : start + PANEL, :])
+    inner = row_dot(coords[begin:end, :], coords[start : start + size, :])
     column = down[begin:end, :]
-    column = jnp.concatenate([column] * (PANEL // LANES), axis=1)
-    power = (2.0 * turn) * inner + column + along[:1, start : start + PANEL]
-    kernel[begin:end, start : start + PANEL] = jnp.exp2(power).astype(jnp.bfloat16)
+    column = jnp.concatenate([column] * (size // LANES), axis=1)
+    power = (2.0 * turn) * inner + column + along[:1, start : start + size]
+    kernel[begin:end, start : start + size] = jnp.exp2(power).astype(jnp.bfloat16)
 
 
 def join(parts):
@@ -199,10 +199,8 @@
     parts[:, :half] = own_parts[...]
     for i in range(half, whole, PANEL):
         scaled_norms(coords, i, down, along, eye)
-    for j in range(0, half, PANEL):
-        kernel_columns(coords, down, along, kernel, half, whole, j)
-    for j in range(half, whole, PANEL):
-        kernel_columns(coords, down, along, kernel, 0, whole, j)
+    kernel_columns(coords, down, along, kernel, half, whole, 0, whole)
+    kernel_columns(coords, down, along, kernel, 0, half, half, half)
     products = [
         own_image[...] + plain_dot(parts[:, half:], kernel[half:, :half]),
         plain_dot(parts[...], kernel[:, half:]),

time: 24.4 us -> 24.4 us (level)
  no operation moved by 1% of the time
where the time goes in v1:
time: 24.4 us; the launch traced here: 24.2 us
  starting transfers between devices  11.2 us (46%)
  waiting for transfers between devices  8.04 us (33%)
  Pallas kernels  2.75 us (11%)
  local copies, waits for them, and re-layouts  1.51 us (6%)
  between operations  0.67 us (3%)
    ppermute x11, starting transfers between devices, swap(): return lax.ppermute(array, AXES, pairs)  11.2 us
    ppermute x11, waiting for transfers between devices, swap(): return lax.ppermute(array, AXES, pairs)  8.04 us
    pallas_call x1, Pallas kernels, whole_local(): pl.pallas_call(functools.partial(solve_kernel, across, rows, len(theirs))...  2.1 us
    unnamed x8, local copies, waits for them, and re-layouts  1.48 us
    pallas_call x1, Pallas kernels, whole_local(): pl.pallas_call(functools.partial(own_kernel, across, rows, len(ours)), ou...  0.56 us
  transfers between devices with their start and end apart: 11, of which 7 were waited for; matrix products, arithmetic and copies ran while one was open for 0% of the time, Pallas kernels for 3%

profile of v1, /device:TPU:0, one launch (start us, length us, event | category | flops | bytes accessed | tf_op | source)
XLA Modules:
  0.0 24.2 jit_solution(5230402268654913958)
XLA Ops:
  0.6 4.1 %collective-permute-start.1 = (bf16[64,128]{1,0:T(8,128)(2,1)}, bf16[64,128]{1,0:T(8,128)(2,1)S(1)}, u32[]{:S(2)}, u32[]{:S(2)}) collective-permute-start(bf16[64,128]{1,0:T(8,128)(2,1)} %points.1), channel_id=1, source_target_pairs={{0,16},{1,17},{2,18},{3,19},{4,20},{5,21},{6,22},{7,23},{8,24},{9,... | collective-permute-start | bytes 49160 | tf_op jit(solution)/shard_map/ppermute | solution.py:239
  4.8 0.0 copy-start
  4.8 0.7 %copy-done = bf16[64,128]{1,0:T(8,128)(2,1)S(1)} copy-done((bf16[64,128]{1,0:T(8,128)(2,1)S(1)}, bf16[64,128]{1,0:T(8,128)(2,1)}, u32[]{:S(2)}) %copy-start) | copy-done | bytes 16408
  5.5 0.0 copy-start.1
  5.5 0.7 %copy-done.1 = f32[64,16]{0,1:T(8,128)S(1)} copy-done((f32[64,16]{0,1:T(8,128)S(1)}, f32[64,16]{0,1:T(8,128)}, u32[]{:S(2)}) %copy-start.1) | copy-done | bytes 4120
  6.2 0.1 shard_map.41
  6.3 1.6 %collective-permute-start = (bf16[80,128]{1,0:T(8,128)(2,1)S(1)}, bf16[80,128]{1,0:T(8,128)(2,1)S(1)}, u32[]{:S(2)}, u32[]{:S(2)}) collective-permute-start(bf16[80,128]{1,0:T(8,128)(2,1)S(1)} %get-tuple-element.12), channel_id=1, source_target_pairs={{0,8},{1,9},{2,10},{3,11},{4,12},{5,13},{6,14},{7,15},{8,0},{9,1},... | collective-permute-start | bytes 61448 | tf_op jit(solution)/shard_map/ppermute | solution.py:239
  7.9 0.0 collective-permute-start.2
  7.9 1.9 %collective-permute-start.3 = (bf16[16,128]{1,0:T(8,128)(2,1)S(1)}, bf16[16,128]{1,0:T(8,128)(2,1)S(1)}, u32[]{:S(2)}, u32[]{:S(2)}) collective-permute-start(bf16[16,128]{1,0:T(8,128)(2,1)S(1)} %get-tuple-element.13), channel_id=1, source_target_pairs={{0,16},{1,17},{2,18},{3,19},{4,20},{5,21},{6,22},{7,23},{8,24},{9,... | collective-permute-start | bytes 12296 | tf_op jit(solution)/shard_map/ppermute | solution.py:239
  9.8 0.3 %collective-permute-done = bf16[80,128]{1,0:T(8,128)(2,1)S(1)} collective-permute-done((bf16[80,128]{1,0:T(8,128)(2,1)S(1)}, bf16[80,128]{1,0:T(8,128)(2,1)S(1)}, u32[]{:S(2)}, u32[]{:S(2)}) %collective-permute-start) | collective-permute-done | bytes 20512 | tf_op jit(solution)/shard_map/ppermute | solution.py:239
  10.1 0.0 collective-permute-done.1
  10.1 3.3 %collective-permute-done.2 = bf16[80,128]{1,0:T(8,128)(2,1)S(1)} collective-permute-done((bf16[80,128]{1,0:T(8,128)(2,1)S(1)}, bf16[80,128]{1,0:T(8,128)(2,1)S(1)}, u32[]{:S(2)}, u32[]{:S(2)}) %collective-permute-start.2) | collective-permute-done | bytes 20512 | tf_op jit(solution)/shard_map/ppermute | solution.py:239
  13.5 0.0 collective-permute-done.3
  13.5 1.6 %collective-permute-start.7 = (bf16[320,128]{1,0:T(8,128)(2,1)S(1)}, bf16[320,128]{1,0:T(8,128)(2,1)S(1)}, u32[]{:S(2)}, u32[]{:S(2)}) collective-permute-start(bf16[320,128]{1,0:T(8,128)(2,1)S(1)} %constant_dynamic-update-slice_fusion.refs_0_), channel_id=1, source_target_pairs={{0,4},{1,5},{2,6},{3,7},{4,0},{5,1},{6,2},{7,3},{8,12},{9,13},{10,... | collective-permute-start | bytes 245768 | tf_op jit(solution)/shard_map/ppermute | solution.py:239
  15.1 1.4 %collective-permute-start.9 = (bf16[256,128]{1,0:T(8,128)(2,1)S(1)}, bf16[256,128]{1,0:T(8,128)(2,1)S(1)}, u32[]{:S(2)}, u32[]{:S(2)}) collective-permute-start(bf16[256,128]{1,0:T(8,128)(2,1)S(1)} %pad_maximum_fusion), channel_id=1, source_target_pairs={{0,5},{1,4},{2,7},{3,6},{4,1},{5,0},{6,3},{7,2},{8,13},{9,12},{10,... | collective-permute-start | bytes 196616 | tf_op jit(solution)/shard_map/ppermute | solution.py:239
  16.5 0.5 %collective-permute-start.5 = (bf16[256,128]{1,0:T(8,128)(2,1)S(1)}, bf16[256,128]{1,0:T(8,128)(2,1)S(1)}, u32[]{:S(2)}, u32[]{:S(2)}) collective-permute-start(bf16[256,128]{1,0:T(8,128)(2,1)S(1)} %pad_maximum_fusion), channel_id=1, source_target_pairs={{0,1},{1,0},{2,3},{3,2},{4,5},{5,4},{6,7},{7,6},{8,9},{9,8},{10,11... | collective-permute-start | bytes 196616 | tf_op jit(solution)/shard_map/ppermute | solution.py:239
  17.1 0.0 collective-permute-start.4
  17.1 0.9 %collective-permute-done.7.refs_2_ = bf16[320,128]{1,0:T(8,128)(2,1)S(1)} collective-permute-done((bf16[320,128]{1,0:T(8,128)(2,1)S(1)}, bf16[320,128]{1,0:T(8,128)(2,1)S(1)}, u32[]{:S(2)}, u32[]{:S(2)}) %collective-permute-start.7) | collective-permute-done | bytes 81952 | tf_op jit(solution)/shard_map/ppermute | solution.py:239
  18.0 0.0 collective-permute-start.8
  18.0 2.2 %collective-permute-done.9.refs_3_ = bf16[256,128]{1,0:T(8,128)(2,1)S(1)} collective-permute-done((bf16[256,128]{1,0:T(8,128)(2,1)S(1)}, bf16[256,128]{1,0:T(8,128)(2,1)S(1)}, u32[]{:S(2)}, u32[]{:S(2)}) %collective-permute-start.9) | collective-permute-done | bytes 65568 | tf_op jit(solution)/shard_map/ppermute | solution.py:239
  20.3 0.0 collective-permute-start.10
  20.3 0.5 %collective-permute-done.5.refs_1_ = bf16[256,128]{1,0:T(8,128)(2,1)S(1)} collective-permute-done((bf16[256,128]{1,0:T(8,128)(2,1)S(1)}, bf16[256,128]{1,0:T(8,128)(2,1)S(1)}, u32[]{:S(2)}, u32[]{:S(2)}) %collective-permute-start.5) | collective-permute-done | bytes 65568 | tf_op jit(solution)/shard_map/ppermute | solution.py:239
  20.8 0.0 collective-permute-start.6
  20.8 0.6 %shard_map.43 = (bf16[512,256]{1,0:T(8,128)(2,1)S(1)}, f32[512,128]{1,0:T(8,128)S(1)}, f32[8,512]{1,0:T(8,128)S(1)}, bf16[512,512]{1,0:T(8,128)(2,1)S(1)}, bf16[...) custom-call(bf16[320,128]{1,0:T(8,128)(2,1)S(1)} %constant_dynamic-update-slice_fusion.refs_0_, ...), custom_call_target="tpu_custom_call" | custom-call | flops 201326592 | bytes 262144 | tf_op jit(solution)/shard_map/pallas_call | solution.py:300
  21.4 0.0 collective-permute-done.4.refs_0_
  21.4 0.1 collective-permute-done.10.refs_3_
  21.5 0.5 %collective-permute-done.6.refs_1_ = bf16[256,128]{1,0:T(8,128)(2,1)S(1)} collective-permute-done((bf16[256,128]{1,0:T(8,128)(2,1)S(1)}, bf16[256,128]{1,0:T(8,128)(2,1)S(1)}, u32[]{:S(2)}, u32[]{:S(2)}) %collective-permute-start.6) | collective-permute-done | bytes 65568 | tf_op jit(solution)/shard_map/ppermute | solution.py:239
  22.0 0.0 collective-permute-done.8.refs_2_
  22.1 2.1 %shard_map.44 = (f32[16,64]{1,0:T(8,128)}, f32[16,64]{1,0:T(8,128)}) custom-call(bf16[320,128]{1,0:T(8,128)(2,1)S(1)} %collective-permute-done.4.refs_0_, bf16[256,128]{1,0:T(8,128)(2,1)S(1)} %collective-permute-done.6.refs_1_, bf16[320,128]{1,0:T(8,128)(2,1)S(1)} %collective-permute-done.8.refs_2_, bf16[256,128]{1,0:T(8,128)(2,1)S(1)} %collective-permute-done.10.refs_3_, ...), custom_call_target="tpu_custom_call" | custom-call | flops 603979776 | bytes 262144 | tf_op jit(solution)/shard_map/pallas_call | solution.py:312
  (10 shorter events, 0.1 us)
Async XLA Ops:
  0.6 9.5 %collective-permute-start.1 = (bf16[64,128]{1,0:T(8,128)(2,1)}, bf16[64,128]{1,0:T(8,128)(2,1)S(1)}, u32[]{:S(2)}, u32[]{:S(2)}) collective-permute-start(bf16[64,128]{1,0:T(8,128)(2,1)} %points.1), channel_id=1, source_target_pairs={{0,16},{1,17},{2,18},{3,19},{4,20},{5,21},{6,22},{7,23},{8,24},{9,... | collective-permute-start | bytes 49160 | tf_op jit(solution)/shard_map/ppermute | solution.py:239
  4.8 0.8 %copy-start = (bf16[64,128]{1,0:T(8,128)(2,1)S(1)}, bf16[64,128]{1,0:T(8,128)(2,1)}, u32[]{:S(2)}) copy-start(bf16[64,128]{1,0:T(8,128)(2,1)} %points.1) | copy-start | bytes 49156
  5.5 0.7 %copy-start.1 = (f32[64,16]{0,1:T(8,128)S(1)}, f32[64,16]{0,1:T(8,128)}, u32[]{:S(2)}) copy-start(f32[64,16]{0,1:T(8,128)} %param.3) | copy-start | bytes 12292
  6.3 3.8 %collective-permute-start = (bf16[80,128]{1,0:T(8,128)(2,1)S(1)}, bf16[80,128]{1,0:T(8,128)(2,1)S(1)}, u32[]{:S(2)}, u32[]{:S(2)}) collective-permute-start(bf16[80,128]{1,0:T(8,128)(2,1)S(1)} %get-tuple-element.12), channel_id=1, source_target_pairs={{0,8},{1,9},{2,10},{3,11},{4,12},{5,13},{6,14},{7,15},{8,0},{9,1},... | collective-permute-start | bytes 61448 | tf_op jit(solution)/shard_map/ppermute | solution.py:239
  7.9 5.6 %collective-permute-start.2 = (bf16[80,128]{1,0:T(8,128)(2,1)S(1)}, bf16[80,128]{1,0:T(8,128)(2,1)S(1)}, u32[]{:S(2)}, u32[]{:S(2)}) collective-permute-start(bf16[80,128]{1,0:T(8,128)(2,1)S(1)} %get-tuple-element.12), channel_id=1, source_target_pairs={{0,24},{1,25},{2,26},{3,27},{4,28},{5,29},{6,30},{7,31},{8,16},{9,... | collective-permute-start | bytes 61448 | tf_op jit(solution)/shard_map/ppermute | solution.py:239
  7.9 5.6 %collective-permute-start.3 = (bf16[16,128]{1,0:T(8,128)(2,1)S(1)}, bf16[16,128]{1,0:T(8,128)(2,1)S(1)}, u32[]{:S(2)}, u32[]{:S(2)}) collective-permute-start(bf16[16,128]{1,0:T(8,128)(2,1)S(1)} %get-tuple-element.13), channel_id=1, source_target_pairs={{0,16},{1,17},{2,18},{3,19},{4,20},{5,21},{6,22},{7,23},{8,24},{9,... | collective-permute-start | bytes 12296 | tf_op jit(solution)/shard_map/ppermute | solution.py:239
  13.5 4.5 %collective-permute-start.7 = (bf16[320,128]{1,0:T(8,128)(2,1)S(1)}, bf16[320,128]{1,0:T(8,128)(2,1)S(1)}, u32[]{:S(2)}, u32[]{:S(2)}) collective-permute-start(bf16[320,128]{1,0:T(8,128)(2,1)S(1)} %constant_dynamic-update-slice_fusion.refs_0_), channel_id=1, source_target_pairs={{0,4},{1,5},{2,6},{3,7},{4,0},{5,1},{6,2},{7,3},{8,12},{9,13},{10,... | collective-permute-start | bytes 245768 | tf_op jit(solution)/shard_map/ppermute | solution.py:239
  15.1 5.2 %collective-permute-start.9 = (bf16[256,128]{1,0:T(8,128)(2,1)S(1)}, bf16[256,128]{1,0:T(8,128)(2,1)S(1)}, u32[]{:S(2)}, u32[]{:S(2)}) collective-permute-start(bf16[256,128]{1,0:T(8,128)(2,1)S(1)} %pad_maximum_fusion), channel_id=1, source_target_pairs={{0,5},{1,4},{2,7},{3,6},{4,1},{5,0},{6,3},{7,2},{8,13},{9,12},{10,... | collective-permute-start | bytes 196616 | tf_op jit(solution)/shard_map/ppermute | solution.py:239
  16.5 4.3 %collective-permute-start.5 = (bf16[256,128]{1,0:T(8,128)(2,1)S(1)}, bf16[256,128]{1,0:T(8,128)(2,1)S(1)}, u32[]{:S(2)}, u32[]{:S(2)}) collective-permute-start(bf16[256,128]{1,0:T(8,128)(2,1)S(1)} %pad_maximum_fusion), channel_id=1, source_target_pairs={{0,1},{1,0},{2,3},{3,2},{4,5},{5,4},{6,7},{7,6},{8,9},{9,8},{10,11... | collective-permute-start | bytes 196616 | tf_op jit(solution)/shard_map/ppermute | solution.py:239
  17.1 4.3 %collective-permute-start.4 = (bf16[320,128]{1,0:T(8,128)(2,1)S(1)}, bf16[320,128]{1,0:T(8,128)(2,1)S(1)}, u32[]{:S(2)}, u32[]{:S(2)}) collective-permute-start(bf16[320,128]{1,0:T(8,128)(2,1)S(1)} %constant_dynamic-update-slice_fusion.refs_0_), channel_id=1, source_target_pairs={{0,2},{1,3},{2,0},{3,1},{4,6},{5,7},{6,4},{7,5},{8,10},{9,11},{10,... | collective-permute-start | bytes 245768 | tf_op jit(solution)/shard_map/ppermute | solution.py:239
  18.0 4.0 %collective-permute-start.8 = (bf16[320,128]{1,0:T(8,128)(2,1)S(1)}, bf16[320,128]{1,0:T(8,128)(2,1)S(1)}, u32[]{:S(2)}, u32[]{:S(2)}) collective-permute-start(bf16[320,128]{1,0:T(8,128)(2,1)S(1)} %collective-permute-done.7.refs_2_), channel_id=1, source_target_pairs={{0,2},{1,3},{2,0},{3,1},{4,6},{5,7},{6,4},{7,5},{8,10},{9,11},{10,... | collective-permute-start | bytes 245768 | tf_op jit(solution)/shard_map/ppermute | solution.py:239
  20.3 1.3 %collective-permute-start.10 = (bf16[256,128]{1,0:T(8,128)(2,1)S(1)}, bf16[256,128]{1,0:T(8,128)(2,1)S(1)}, u32[]{:S(2)}, u32[]{:S(2)}) collective-permute-start(bf16[256,128]{1,0:T(8,128)(2,1)S(1)} %collective-permute-done.9.refs_3_), channel_id=1, source_target_pairs={{0,2},{1,3},{2,0},{3,1},{4,6},{5,7},{6,4},{7,5},{8,10},{9,11},{10,... | collective-permute-start | bytes 196616 | tf_op jit(solution)/shard_map/ppermute | solution.py:239
  20.8 1.3 %collective-permute-start.6 = (bf16[256,128]{1,0:T(8,128)(2,1)S(1)}, bf16[256,128]{1,0:T(8,128)(2,1)S(1)}, u32[]{:S(2)}, u32[]{:S(2)}) collective-permute-start(bf16[256,128]{1,0:T(8,128)(2,1)S(1)} %collective-permute-done.5.refs_1_), channel_id=1, source_target_pairs={{0,2},{1,3},{2,0},{3,1},{4,6},{5,7},{6,4},{7,5},{8,10},{9,11},{10,... | collective-permute-start | bytes 196616 | tf_op jit(solution)/shard_map/ppermute | solution.py:239

commit v2 on v1

--- a/solution.py
+++ b/solution.py
@@ -93,7 +93,7 @@
 
 AXES = ("gx", "gy", "af")
 LANES = 128
-PANEL = 4 * LANES
+PANEL = 2 * LANES
 EYE_COST = pl.CostEstimate(flops=20000000, transcendentals=0, bytes_accessed=65536)
 KERNEL_BYTES = 8 * 1024 * 1024
 
@@ -178,9 +178,8 @@
     half = coords.shape[0]
     for i in range(0, half, PANEL):
         scaled_norms(coords, i, down, along, eye)
-    for j in range(0, half, PANEL):
-        kernel_columns(coords, down, along, kernel, 0, half, j)
-        image[:, j : j + PANEL] = plain_dot(parts[...], kernel[:, j : j + PANEL])
+    kernel_columns(coords, down, along, kernel, 0, half, 0, half)
+    image[...] = plain_dot(parts[...], kernel[...])
 
 
 def solve_kernel(blocks, rows, count, *refs):

time: 24.4 us -> 24.4 us (level)
  no operation moved by 1% of the time
where the time goes in v2:
time: 24.4 us; the launch traced here: 24.2 us
  starting transfers between devices  11.2 us (46%)
  waiting for transfers between devices  8.04 us (33%)
  Pallas kernels  2.75 us (11%)
  local copies, waits for them, and re-layouts  1.51 us (6%)
  between operations  0.67 us (3%)
    ppermute x11, starting transfers between devices, swap(): return lax.ppermute(array, AXES, pairs)  11.2 us
    ppermute x11, waiting for transfers between devices, swap(): return lax.ppermute(array, AXES, pairs)  8.04 us
    pallas_call x1, Pallas kernels, whole_local(): pl.pallas_call(functools.partial(solve_kernel, across, rows, len(theirs))...  2.1 us
    unnamed x8, local copies, waits for them, and re-layouts  1.48 us
    pallas_call x1, Pallas kernels, whole_local(): pl.pallas_call(functools.partial(own_kernel, across, rows, len(ours)), ou...  0.56 us
  transfers between devices with their start and end apart: 11, of which 7 were waited for; matrix products, arithmetic and copies ran while one was open for 0% of the time, Pallas kernels for 3%

profile of v2, /device:TPU:0, one launch (start us, length us, event | category | flops | bytes accessed | tf_op | source)
XLA Modules:
  0.0 24.2 jit_solution(15229379012945536189)
XLA Ops:
  0.6 4.1 %collective-permute-start.1 = (bf16[64,128]{1,0:T(8,128)(2,1)}, bf16[64,128]{1,0:T(8,128)(2,1)S(1)}, u32[]{:S(2)}, u32[]{:S(2)}) collective-permute-start(bf16[64,128]{1,0:T(8,128)(2,1)} %points.1), channel_id=1, source_target_pairs={{0,16},{1,17},{2,18},{3,19},{4,20},{5,21},{6,22},{7,23},{8,24},{9,... | collective-permute-start | bytes 49160 | tf_op jit(solution)/shard_map/ppermute | solution.py:238
  4.8 0.0 copy-start
  4.8 0.7 %copy-done = bf16[64,128]{1,0:T(8,128)(2,1)S(1)} copy-done((bf16[64,128]{1,0:T(8,128)(2,1)S(1)}, bf16[64,128]{1,0:T(8,128)(2,1)}, u32[]{:S(2)}) %copy-start) | copy-done | bytes 16408
  5.5 0.0 copy-start.1
  5.5 0.7 %copy-done.1 = f32[64,16]{0,1:T(8,128)S(1)} copy-done((f32[64,16]{0,1:T(8,128)S(1)}, f32[64,16]{0,1:T(8,128)}, u32[]{:S(2)}) %copy-start.1) | copy-done | bytes 4120
  6.2 0.1 shard_map.41
  6.3 1.6 %collective-permute-start = (bf16[80,128]{1,0:T(8,128)(2,1)S(1)}, bf16[80,128]{1,0:T(8,128)(2,1)S(1)}, u32[]{:S(2)}, u32[]{:S(2)}) collective-permute-start(bf16[80,128]{1,0:T(8,128)(2,1)S(1)} %get-tuple-element.12), channel_id=1, source_target_pairs={{0,8},{1,9},{2,10},{3,11},{4,12},{5,13},{6,14},{7,15},{8,0},{9,1},... | collective-permute-start | bytes 61448 | tf_op jit(solution)/shard_map/ppermute | solution.py:238
  7.9 0.0 collective-permute-start.2
  7.9 1.9 %collective-permute-start.3 = (bf16[16,128]{1,0:T(8,128)(2,1)S(1)}, bf16[16,128]{1,0:T(8,128)(2,1)S(1)}, u32[]{:S(2)}, u32[]{:S(2)}) collective-permute-start(bf16[16,128]{1,0:T(8,128)(2,1)S(1)} %get-tuple-element.13), channel_id=1, source_target_pairs={{0,16},{1,17},{2,18},{3,19},{4,20},{5,21},{6,22},{7,23},{8,24},{9,... | collective-permute-start | bytes 12296 | tf_op jit(solution)/shard_map/ppermute | solution.py:238
  9.8 0.3 %collective-permute-done = bf16[80,128]{1,0:T(8,128)(2,1)S(1)} collective-permute-done((bf16[80,128]{1,0:T(8,128)(2,1)S(1)}, bf16[80,128]{1,0:T(8,128)(2,1)S(1)}, u32[]{:S(2)}, u32[]{:S(2)}) %collective-permute-start) | collective-permute-done | bytes 20512 | tf_op jit(solution)/shard_map/ppermute | solution.py:238
  10.1 0.0 collective-permute-done.1
  10.1 3.3 %collective-permute-done.2 = bf16[80,128]{1,0:T(8,128)(2,1)S(1)} collective-permute-done((bf16[80,128]{1,0:T(8,128)(2,1)S(1)}, bf16[80,128]{1,0:T(8,128)(2,1)S(1)}, u32[]{:S(2)}, u32[]{:S(2)}) %collective-permute-start.2) | collective-permute-done | bytes 20512 | tf_op jit(solution)/shard_map/ppermute | solution.py:238
  13.5 0.0 collective-permute-done.3
  13.5 1.6 %collective-permute-start.7 = (bf16[320,128]{1,0:T(8,128)(2,1)S(1)}, bf16[320,128]{1,0:T(8,128)(2,1)S(1)}, u32[]{:S(2)}, u32[]{:S(2)}) collective-permute-start(bf16[320,128]{1,0:T(8,128)(2,1)S(1)} %constant_dynamic-update-slice_fusion.refs_0_), channel_id=1, source_target_pairs={{0,4},{1,5},{2,6},{3,7},{4,0},{5,1},{6,2},{7,3},{8,12},{9,13},{10,... | collective-permute-start | bytes 245768 | tf_op jit(solution)/shard_map/ppermute | solution.py:238
  15.1 1.4 %collective-permute-start.9 = (bf16[256,128]{1,0:T(8,128)(2,1)S(1)}, bf16[256,128]{1,0:T(8,128)(2,1)S(1)}, u32[]{:S(2)}, u32[]{:S(2)}) collective-permute-start(bf16[256,128]{1,0:T(8,128)(2,1)S(1)} %pad_maximum_fusion), channel_id=1, source_target_pairs={{0,5},{1,4},{2,7},{3,6},{4,1},{5,0},{6,3},{7,2},{8,13},{9,12},{10,... | collective-permute-start | bytes 196616 | tf_op jit(solution)/shard_map/ppermute | solution.py:238
  16.5 0.5 %collective-permute-start.5 = (bf16[256,128]{1,0:T(8,128)(2,1)S(1)}, bf16[256,128]{1,0:T(8,128)(2,1)S(1)}, u32[]{:S(2)}, u32[]{:S(2)}) collective-permute-start(bf16[256,128]{1,0:T(8,128)(2,1)S(1)} %pad_maximum_fusion), channel_id=1, source_target_pairs={{0,1},{1,0},{2,3},{3,2},{4,5},{5,4},{6,7},{7,6},{8,9},{9,8},{10,11... | collective-permute-start | bytes 196616 | tf_op jit(solution)/shard_map/ppermute | solution.py:238
  17.1 0.0 collective-permute-start.4
  17.1 0.9 %collective-permute-done.7.refs_2_ = bf16[320,128]{1,0:T(8,128)(2,1)S(1)} collective-permute-done((bf16[320,128]{1,0:T(8,128)(2,1)S(1)}, bf16[320,128]{1,0:T(8,128)(2,1)S(1)}, u32[]{:S(2)}, u32[]{:S(2)}) %collective-permute-start.7) | collective-permute-done | bytes 81952 | tf_op jit(solution)/shard_map/ppermute | solution.py:238
  18.0 0.0 collective-permute-start.8
  18.0 2.2 %collective-permute-done.9.refs_3_ = bf16[256,128]{1,0:T(8,128)(2,1)S(1)} collective-permute-done((bf16[256,128]{1,0:T(8,128)(2,1)S(1)}, bf16[256,128]{1,0:T(8,128)(2,1)S(1)}, u32[]{:S(2)}, u32[]{:S(2)}) %collective-permute-start.9) | collective-permute-done | bytes 65568 | tf_op jit(solution)/shard_map/ppermute | solution.py:238
  20.3 0.0 collective-permute-start.10
  20.3 0.5 %collective-permute-done.5.refs_1_ = bf16[256,128]{1,0:T(8,128)(2,1)S(1)} collective-permute-done((bf16[256,128]{1,0:T(8,128)(2,1)S(1)}, bf16[256,128]{1,0:T(8,128)(2,1)S(1)}, u32[]{:S(2)}, u32[]{:S(2)}) %collective-permute-start.5) | collective-permute-done | bytes 65568 | tf_op jit(solution)/shard_map/ppermute | solution.py:238
  20.8 0.0 collective-permute-start.6
  20.8 0.6 %shard_map.43 = (bf16[512,256]{1,0:T(8,128)(2,1)S(1)}, f32[512,128]{1,0:T(8,128)S(1)}, f32[8,512]{1,0:T(8,128)S(1)}, bf16[512,512]{1,0:T(8,128)(2,1)S(1)}, bf16[...) custom-call(bf16[320,128]{1,0:T(8,128)(2,1)S(1)} %constant_dynamic-update-slice_fusion.refs_0_, ...), custom_call_target="tpu_custom_call" | custom-call | flops 201326592 | bytes 262144 | tf_op jit(solution)/shard_map/pallas_call | solution.py:299
  21.4 0.0 collective-permute-done.4.refs_0_
  21.4 0.1 collective-permute-done.10.refs_3_
  21.5 0.5 %collective-permute-done.6.refs_1_ = bf16[256,128]{1,0:T(8,128)(2,1)S(1)} collective-permute-done((bf16[256,128]{1,0:T(8,128)(2,1)S(1)}, bf16[256,128]{1,0:T(8,128)(2,1)S(1)}, u32[]{:S(2)}, u32[]{:S(2)}) %collective-permute-start.6) | collective-permute-done | bytes 65568 | tf_op jit(solution)/shard_map/ppermute | solution.py:238
  22.0 0.0 collective-permute-done.8.refs_2_
  22.1 2.1 %shard_map.44 = (f32[16,64]{1,0:T(8,128)}, f32[16,64]{1,0:T(8,128)}) custom-call(bf16[320,128]{1,0:T(8,128)(2,1)S(1)} %collective-permute-done.4.refs_0_, bf16[256,128]{1,0:T(8,128)(2,1)S(1)} %collective-permute-done.6.refs_1_, bf16[320,128]{1,0:T(8,128)(2,1)S(1)} %collective-permute-done.8.refs_2_, bf16[256,128]{1,0:T(8,128)(2,1)S(1)} %collective-permute-done.10.refs_3_, ...), custom_call_target="tpu_custom_call" | custom-call | flops 603979776 | bytes 262144 | tf_op jit(solution)/shard_map/pallas_call | solution.py:311
  (10 shorter events, 0.1 us)
Async XLA Ops:
  0.6 9.5 %collective-permute-start.1 = (bf16[64,128]{1,0:T(8,128)(2,1)}, bf16[64,128]{1,0:T(8,128)(2,1)S(1)}, u32[]{:S(2)}, u32[]{:S(2)}) collective-permute-start(bf16[64,128]{1,0:T(8,128)(2,1)} %points.1), channel_id=1, source_target_pairs={{0,16},{1,17},{2,18},{3,19},{4,20},{5,21},{6,22},{7,23},{8,24},{9,... | collective-permute-start | bytes 49160 | tf_op jit(solution)/shard_map/ppermute | solution.py:238
  4.8 0.8 %copy-start = (bf16[64,128]{1,0:T(8,128)(2,1)S(1)}, bf16[64,128]{1,0:T(8,128)(2,1)}, u32[]{:S(2)}) copy-start(bf16[64,128]{1,0:T(8,128)(2,1)} %points.1) | copy-start | bytes 49156
  5.5 0.7 %copy-start.1 = (f32[64,16]{0,1:T(8,128)S(1)}, f32[64,16]{0,1:T(8,128)}, u32[]{:S(2)}) copy-start(f32[64,16]{0,1:T(8,128)} %param.3) | copy-start | bytes 12292
  6.3 3.8 %collective-permute-start = (bf16[80,128]{1,0:T(8,128)(2,1)S(1)}, bf16[80,128]{1,0:T(8,128)(2,1)S(1)}, u32[]{:S(2)}, u32[]{:S(2)}) collective-permute-start(bf16[80,128]{1,0:T(8,128)(2,1)S(1)} %get-tuple-element.12), channel_id=1, source_target_pairs={{0,8},{1,9},{2,10},{3,11},{4,12},{5,13},{6,14},{7,15},{8,0},{9,1},... | collective-permute-start | bytes 61448 | tf_op jit(solution)/shard_map/ppermute | solution.py:238
  7.9 5.6 %collective-permute-start.2 = (bf16[80,128]{1,0:T(8,128)(2,1)S(1)}, bf16[80,128]{1,0:T(8,128)(2,1)S(1)}, u32[]{:S(2)}, u32[]{:S(2)}) collective-permute-start(bf16[80,128]{1,0:T(8,128)(2,1)S(1)} %get-tuple-element.12), channel_id=1, source_target_pairs={{0,24},{1,25},{2,26},{3,27},{4,28},{5,29},{6,30},{7,31},{8,16},{9,... | collective-permute-start | bytes 61448 | tf_op jit(solution)/shard_map/ppermute | solution.py:238
  7.9 5.6 %collective-permute-start.3 = (bf16[16,128]{1,0:T(8,128)(2,1)S(1)}, bf16[16,128]{1,0:T(8,128)(2,1)S(1)}, u32[]{:S(2)}, u32[]{:S(2)}) collective-permute-start(bf16[16,128]{1,0:T(8,128)(2,1)S(1)} %get-tuple-element.13), channel_id=1, source_target_pairs={{0,16},{1,17},{2,18},{3,19},{4,20},{5,21},{6,22},{7,23},{8,24},{9,... | collective-permute-start | bytes 12296 | tf_op jit(solution)/shard_map/ppermute | solution.py:238
  13.5 4.5 %collective-permute-start.7 = (bf16[320,128]{1,0:T(8,128)(2,1)S(1)}, bf16[320,128]{1,0:T(8,128)(2,1)S(1)}, u32[]{:S(2)}, u32[]{:S(2)}) collective-permute-start(bf16[320,128]{1,0:T(8,128)(2,1)S(1)} %constant_dynamic-update-slice_fusion.refs_0_), channel_id=1, source_target_pairs={{0,4},{1,5},{2,6},{3,7},{4,0},{5,1},{6,2},{7,3},{8,12},{9,13},{10,... | collective-permute-start | bytes 245768 | tf_op jit(solution)/shard_map/ppermute | solution.py:238
  15.1 5.2 %collective-permute-start.9 = (bf16[256,128]{1,0:T(8,128)(2,1)S(1)}, bf16[256,128]{1,0:T(8,128)(2,1)S(1)}, u32[]{:S(2)}, u32[]{:S(2)}) collective-permute-start(bf16[256,128]{1,0:T(8,128)(2,1)S(1)} %pad_maximum_fusion), channel_id=1, source_target_pairs={{0,5},{1,4},{2,7},{3,6},{4,1},{5,0},{6,3},{7,2},{8,13},{9,12},{10,... | collective-permute-start | bytes 196616 | tf_op jit(solution)/shard_map/ppermute | solution.py:238
  16.5 4.3 %collective-permute-start.5 = (bf16[256,128]{1,0:T(8,128)(2,1)S(1)}, bf16[256,128]{1,0:T(8,128)(2,1)S(1)}, u32[]{:S(2)}, u32[]{:S(2)}) collective-permute-start(bf16[256,128]{1,0:T(8,128)(2,1)S(1)} %pad_maximum_fusion), channel_id=1, source_target_pairs={{0,1},{1,0},{2,3},{3,2},{4,5},{5,4},{6,7},{7,6},{8,9},{9,8},{10,11... | collective-permute-start | bytes 196616 | tf_op jit(solution)/shard_map/ppermute | solution.py:238
  17.1 4.3 %collective-permute-start.4 = (bf16[320,128]{1,0:T(8,128)(2,1)S(1)}, bf16[320,128]{1,0:T(8,128)(2,1)S(1)}, u32[]{:S(2)}, u32[]{:S(2)}) collective-permute-start(bf16[320,128]{1,0:T(8,128)(2,1)S(1)} %constant_dynamic-update-slice_fusion.refs_0_), channel_id=1, source_target_pairs={{0,2},{1,3},{2,0},{3,1},{4,6},{5,7},{6,4},{7,5},{8,10},{9,11},{10,... | collective-permute-start | bytes 245768 | tf_op jit(solution)/shard_map/ppermute | solution.py:238
  18.0 4.0 %collective-permute-start.8 = (bf16[320,128]{1,0:T(8,128)(2,1)S(1)}, bf16[320,128]{1,0:T(8,128)(2,1)S(1)}, u32[]{:S(2)}, u32[]{:S(2)}) collective-permute-start(bf16[320,128]{1,0:T(8,128)(2,1)S(1)} %collective-permute-done.7.refs_2_), channel_id=1, source_target_pairs={{0,2},{1,3},{2,0},{3,1},{4,6},{5,7},{6,4},{7,5},{8,10},{9,11},{10,... | collective-permute-start | bytes 245768 | tf_op jit(solution)/shard_map/ppermute | solution.py:238
  20.3 1.3 %collective-permute-start.10 = (bf16[256,128]{1,0:T(8,128)(2,1)S(1)}, bf16[256,128]{1,0:T(8,128)(2,1)S(1)}, u32[]{:S(2)}, u32[]{:S(2)}) collective-permute-start(bf16[256,128]{1,0:T(8,128)(2,1)S(1)} %collective-permute-done.9.refs_3_), channel_id=1, source_target_pairs={{0,2},{1,3},{2,0},{3,1},{4,6},{5,7},{6,4},{7,5},{8,10},{9,11},{10,... | collective-permute-start | bytes 196616 | tf_op jit(solution)/shard_map/ppermute | solution.py:238
  20.8 1.3 %collective-permute-start.6 = (bf16[256,128]{1,0:T(8,128)(2,1)S(1)}, bf16[256,128]{1,0:T(8,128)(2,1)S(1)}, u32[]{:S(2)}, u32[]{:S(2)}) collective-permute-start(bf16[256,128]{1,0:T(8,128)(2,1)S(1)} %collective-permute-done.5.refs_1_), channel_id=1, source_target_pairs={{0,2},{1,3},{2,0},{3,1},{4,6},{5,7},{6,4},{7,5},{8,10},{9,11},{10,... | collective-permute-start | bytes 196616 | tf_op jit(solution)/shard_map/ppermute | solution.py:238
